TPU v7x, 32 devices: a whole 2x2x4 slice. The times are simulated.
32 devices in a mesh: replica: 16 (over z, y, core), shard: 2 (over x).
Axes of the slice: x: 2, y: 2, z: 4, core: 2. Of those that a mesh axis runs over, the one named last changes fastest.
Arguments:
- weight: bfloat16 [256, 8192], P(None, 'shard'), may hold values from -6 to 6
- momentum: float32 [16, 256, 8192], P('replica', None, 'shard'), may hold values from -6 to 6
- grad: bfloat16 [16, 256, 8192], P('replica', None, 'shard'), may hold values from -6 to 6
- positions: int32 [16, 4, 128, 32], P('replica', None, 'shard'), may hold values from 0 to 4095, as said below
Outputs:
- kept_state: float32 [16, 256, 8192], P('replica', None, 'shard')
- direction: bfloat16 [256, 8192], P(None, 'shard')
- new_weight: bfloat16 [256, 8192], replicated
Inputs may be any that keep to these rules, and one draw needn't show every extreme that they name: The 32 positions of one block on one replica are distinct; replicas choose independently.
All inputs are finite; a program needn't handle non-finite values.
Results may differ from a plain program's by a relative error of at most 0.001.
Values may be sent and summed in bfloat16 or wider, within the bound.
A program may use at most 128 MiB of HBM per device.

v0:
```python
import math

import jax
import jax.numpy as jnp
from jax import lax
from jax.sharding import PartitionSpec as P

GROUP = 64


beta_decay = 0.9
step_rate = 0.02


def dct_basis():
    freq = jnp.arange(GROUP, dtype=jnp.float32)[:, None]
    cells = jnp.arange(GROUP, dtype=jnp.float32)[None, :]
    scales = jnp.where(freq == 0, math.sqrt(1.0 / GROUP), math.sqrt(2.0 / GROUP))
    return scales * jnp.cos(math.pi * (2.0 * cells + 1.0) * freq / (2.0 * GROUP))


def basis_rows(index, basis_table):
    one_hot = (index[..., None] == jnp.arange(GROUP, dtype=jnp.int32)).astype(jnp.float32)
    return jnp.einsum("xyka,ai->xyki", one_hot, basis_table, precision=lax.Precision.HIGHEST)


def extract(field, pos_table, basis_table):
    row_blocks, col_blocks = (pos_table.shape[0], pos_table.shape[1])
    left_rows = basis_rows(pos_table // GROUP, basis_table)
    right_rows = basis_rows(pos_table % GROUP, basis_table)
    block_view = field.reshape(row_blocks, GROUP, col_blocks, GROUP)
    inner_prod = jnp.einsum(
        "xyki,xiyj->xykj", left_rows, block_view, precision=lax.Precision.HIGHEST
    )
    return jnp.sum(inner_prod * right_rows, axis=-1)


def expand(values, pos_table, basis_table):
    row_blocks, col_blocks = (pos_table.shape[0], pos_table.shape[1])
    left_rows = basis_rows(pos_table // GROUP, basis_table)
    right_rows = basis_rows(pos_table % GROUP, basis_table)
    dense = jnp.einsum(
        "xyki,xyk,xykj->xiyj", left_rows, values, right_rows, precision=lax.Precision.HIGHEST
    )
    return dense.reshape(row_blocks * GROUP, col_blocks * GROUP)


def fill_grid(values, pos_table):
    row_blocks, col_blocks = (pos_table.shape[0], pos_table.shape[1])
    row_index = jnp.arange(row_blocks, dtype=jnp.int32)[:, None, None]
    col_index = jnp.arange(col_blocks, dtype=jnp.int32)[None, :, None]
    flat = jnp.zeros((row_blocks, col_blocks, GROUP * GROUP), jnp.float32)
    return flat.at[row_index, col_index, pos_table].add(values)


def decode(grid, basis_table):
    row_blocks, col_blocks = (grid.shape[0], grid.shape[1])
    square = grid.reshape(row_blocks, col_blocks, GROUP, GROUP)
    dense = jnp.einsum(
        "ai,xyab,bj->xiyj", basis_table, square, basis_table, precision=lax.Precision.HIGHEST
    )
    return dense.reshape(row_blocks * GROUP, col_blocks * GROUP)


def per_device(weight, momentum, grad, positions):
    basis_table = dct_basis()
    own_pos = positions[0]
    moved = beta_decay * momentum[0] + grad[0].astype(jnp.float32)
    picked = extract(moved, own_pos, basis_table)
    kept_state = moved - expand(picked, own_pos, basis_table)
    summed = lax.psum(fill_grid(picked, own_pos), "replica")
    smooth = jnp.tanh(decode(summed, basis_table))
    updated = (weight.astype(jnp.float32) - step_rate * smooth).astype(jnp.bfloat16)
    new_weight = lax.all_gather(updated, "shard", axis=1, tiled=True)
    direction = smooth.astype(jnp.bfloat16)
    return (kept_state[None], direction, new_weight)


def solution(mesh):
    in_specs = (
        P(None, "shard"),
        P("replica", None, "shard"),
        P("replica", None, "shard"),
        P("replica", None, "shard", None),
    )
    out_specs = (P("replica", None, "shard"), P(None, "shard"), P())
    return jax.shard_map(
        per_device, mesh=mesh, in_specs=in_specs, out_specs=out_specs, check_vma=False
    )
```

profile of v0, /device:TPU:15, one launch (start us, length us, event | category | flops | bytes accessed | tf_op | source)
XLA Modules:
  0.0 400.5 jit_solution(15085525133394134084)
XLA Ops:
  7.2 0.0 all-reduce.2.cloned.1.call-start
  7.2 0.9 add_select_fusion.1
  8.1 0.9 compare_select_fusion
  9.0 7.9 %fusion.3 = f32[4,64,32,64]{1,3,2,0:T(8,128)} fusion(s32[4,64,32]{1,2,0:T(8,128)S(1)} %get-tuple-element.6, f32[64]{0:T(128)S(1)} %get-tuple-element.8, f32[64]{0:T(128)S(1)} %get-tuple-element.7), kind=kOutput, calls=%fused_computation.11 | convolution fusion | flops 403189760 | bytes 2130432 | tf_op jit(solution)/shard_map/xyka,ai->xyki/dot_general | solution.py:24
  16.9 6.2 %copy.16 = f32[4,64,32,64]{3,2,1,0:T(8,128)} copy(f32[4,64,32,64]{1,3,2,0:T(8,128)} %fusion.3) | data formatting | bytes 4194304 | tf_op jit(solution)/shard_map/xyka,ai->xyki/dot_general | solution.py:24
  23.1 0.0 copy-start.1
  23.1 0.0 copy-start.2
  23.1 1.4 iota_compare_fusion.1
  24.5 3.9 fusion.4
  28.4 0.0 copy-done.1
  28.4 0.0 copy-done.2
  28.4 2.7 convert_add_fusion
  31.1 0.0 copy-start.4
  31.1 0.0 copy-start.5
  31.1 7.9 %add.65 = f32[4,64,64,64]{3,2,1,0:T(8,128)} reshape(f32[1,256,4096]{2,1,0:T(8,128)} %convert_add_fusion) | data formatting | bytes 8388608 | tf_op jit(solution)/shard_map/add | solution.py:68
  39.0 0.0 copy-done.4
  39.0 0.1 and_reduce_fusion
  39.2 0.0 copy-done.5
  39.2 0.1 multiply_reduce_fusion.1
  39.3 0.1 copy.21
  39.4 0.1 reshape.129
  39.5 17.1 %multiply_reduce_fusion = f32[4,64,32]{2,1,0:T(8,128)S(1)} fusion(f32[4,64,32,64]{3,2,1,0:T(8,128)} %copy.16, f32[4,64,32,64]{3,2,1,0:T(8,128)} %fusion.4, f32[4,64,64,64]{3,2,1,0:T(8,128)} %add.65), kind=kOutput, calls=%fused_computation.7 | convolution fusion | flops 403693568 | bytes 8421376 | tf_op jit(solution)/shard_map/xyki,xiyj->xykj/dot_general | solution.py:32
  56.6 0.1 reshape.131
  56.7 45.4 %scatter_custom_fusion = f32[1048576]{0:T(1024)} fusion(s32[8192]{0:T(1024)S(1)} %reshape.129, f32[8192]{0:T(1024)S(1)} %reshape.131, f32[]{:T(128)} %constant.53.clone.1), kind=kCustom, calls=%fused_computation.15 | custom fusion | flops 8192 | bytes 4194308
  102.1 7.0 %reshape.123 = f32[4,64,64,64]{3,2,1,0:T(8,128)} reshape(f32[1048576]{0:T(1024)} %scatter_custom_fusion) | data formatting | bytes 8388608 | tf_op jit(solution)/shard_map/reshape | solution.py:58
  109.1 0.0 all-reduce.2.cloned.1.call-update
  109.1 0.0 all-gather.2.cloned.1.call-start
  109.2 170.8 %all-reduce.2.cloned.1.call-done = f32[4,64,64,64]{3,2,1,0:T(8,128)} async-done(((f32[4,64,64,64]{3,2,1,0:T(8,128)}), f32[4,64,64,64]{3,2,1,0:T(8,128)}) %all-reduce.2.cloned.1.call-update) | async-done | bytes 4194320 | tf_op jit(solution)/shard_map/psum | solution.py:71
  279.9 11.1 %fusion.17 = f32[4,64,64,64]{2,3,1,0:T(8,128)S(1)} fusion(f32[4,64,64,64]{3,2,1,0:T(8,128)} %all-reduce.2.cloned.1.call-done, f32[64]{0:T(128)S(1)} %get-tuple-element.8, f32[64]{0:T(128)S(1)} %get-tuple-element.7), kind=kOutput, calls=%fused_computation.36 | convolution fusion | flops 805318656 | bytes 8389120 | tf_op jit(solution)/shard_map/ai,xyab,bj->xiyj/dot_general | solution.py:59
  291.0 12.8 %multiply_bitcast_fusion = (f32[4,64,64,64]{3,1,2,0:T(8,128)S(1)}, bf16[4,64,64,64]{3,1,2,0:T(8,128)(2,1)}) fusion(f32[4,64,64,64]{2,3,1,0:T(8,128)S(1)} %fusion.17, f32[64]{0:T(128)S(1)} %get-tuple-element.8, f32[64]{0:T(128)S(1)} %get-tuple-element.7), kind=kOutput, calls=%fused_computation.3 | convolution fusion | flops 807415808 | bytes 10486272 | tf_op jit(solution)/shard_map/ai,xyab,bj->xiyj/dot_general | solution.py:59
  303.8 8.1 %copy.23 = f32[4,64,64,64]{3,2,1,0:T(8,128)} copy(f32[4,64,64,64]{3,1,2,0:T(8,128)S(1)} %get-tuple-element.3) | data formatting | bytes 8388608 | tf_op jit(solution)/shard_map/mul | solution.py:73
  311.9 0.0 copy-start.3
  311.9 8.0 %mul.124 = f32[256,4096]{1,0:T(8,128)} reshape(f32[4,64,64,64]{3,2,1,0:T(8,128)} %copy.23) | data formatting | bytes 8388608 | tf_op jit(solution)/shard_map/mul | solution.py:73
  320.0 0.0 copy-done.3
  320.0 4.1 %subtract_convert_fusion = bf16[256,4096]{1,0:T(8,128)(2,1)} fusion(f32[256,4096]{1,0:T(8,128)} %mul.124, bf16[256,4096]{1,0:T(8,128)(2,1)S(1)} %copy-done.3), kind=kLoop, calls=%fused_computation.6 | loop fusion | flops 3145728 | bytes 8388608 | tf_op jit(solution)/shard_map/convert_element_type | solution.py:73
  324.1 0.0 all-gather.2.cloned.1.call-update
  324.1 0.1 copy.17
  324.2 5.2 %broadcast_multiply_fusion = f32[4,64,32,64]{1,3,2,0:T(8,128)} fusion(f32[4,64,32,64]{1,3,2,0:T(8,128)} %fusion.3, f32[4,64,32]{1,2,0:T(8,128)S(1)} %copy.17), kind=kLoop, calls=%fused_computation.17 | loop fusion | flops 524288 | bytes 4227072 | tf_op jit(solution)/shard_map/xyki,xyk,xykj->xiyj/dot_general | solution.py:42
  329.4 6.5 %copy.18 = f32[4,64,32,64]{3,2,1,0:T(8,128)} copy(f32[4,64,32,64]{1,3,2,0:T(8,128)} %broadcast_multiply_fusion) | data formatting | bytes 4194304 | tf_op jit(solution)/shard_map/xyki,xyk,xykj->xiyj/dot_general | solution.py:42
  335.9 18.5 %convolution_bitcast_fusion = f32[4,64,64,64]{1,3,2,0:T(8,128)} fusion(f32[4,64,32,64]{3,2,1,0:T(8,128)} %copy.18, f32[4,64,32,64]{3,2,1,0:T(8,128)} %fusion.4), kind=kOutput, calls=%fused_computation.14 | convolution fusion | flops 402653184 | bytes 8388608 | tf_op jit(solution)/shard_map/xyki,xyk,xykj->xiyj/dot_general | solution.py:42
  354.4 8.7 %copy.20 = f32[4,64,64,64]{3,2,1,0:T(8,128)} copy(f32[4,64,64,64]{1,3,2,0:T(8,128)} %convolution_bitcast_fusion) | data formatting | bytes 8388608 | tf_op jit(solution)/shard_map/xyki,xyk,xykj->xiyj/transpose | solution.py:42
  363.1 7.9 %reshape.122 = f32[1,256,4096]{2,1,0:T(8,128)} reshape(f32[4,64,64,64]{3,2,1,0:T(8,128)} %copy.20) | data formatting | bytes 8388608 | tf_op jit(solution)/shard_map/reshape | solution.py:45
  371.0 0.0 copy-start
  371.0 6.3 %sub.16 = f32[1,256,4096]{2,1,0:T(8,128)} subtract(f32[1,256,4096]{2,1,0:T(8,128)} %convert_add_fusion, f32[1,256,4096]{2,1,0:T(8,128)} %reshape.122) | non-fusion elementwise | flops 1048576 | bytes 12582912 | tf_op jit(solution)/shard_map/sub | solution.py:70
  377.3 0.0 copy-done
  377.3 4.7 %copy.22 = bf16[4,64,64,64]{3,2,1,0:T(8,128)(2,1)} copy(bf16[4,64,64,64]{3,1,2,0:T(8,128)(2,1)S(1)} %copy-done) | data formatting | bytes 4194304 | tf_op jit(solution)/shard_map/convert_element_type | solution.py:75
  382.0 6.6 %convert_element_type.28 = bf16[256,4096]{1,0:T(8,128)(2,1)} reshape(bf16[4,64,64,64]{3,2,1,0:T(8,128)(2,1)} %copy.22) | data formatting | bytes 4194304 | tf_op jit(solution)/shard_map/convert_element_type | solution.py:75
  388.6 0.0 all-gather.2.cloned.1.call-done
  388.6 4.6 %copy.38 = bf16[256,8192]{1,0:T(8,128)(2,1)} copy(bf16[256,8192]{1,0:T(8,128)(2,1)} %all-gather.2.cloned.1.call-done) | data formatting | bytes 8388608
  (4 shorter events, 0.0 us)
Async XLA Ops:
  7.2 272.8 %all-reduce.2.cloned.1.call-start = ((), (), s32[]{:S(2)}) async-start(), calls=%async_computation | async-start | bytes 16777216 | tf_op jit(solution)/shard_map/psum | solution.py:71
  23.1 5.3 %copy-start.1 = (f32[1,256,4096]{2,1,0:T(8,128)S(1)}, f32[1,256,4096]{2,1,0:T(8,128)}, u32[]{:S(2)}) copy-start(f32[1,256,4096]{2,1,0:T(8,128)} %param.5) | copy-start | bytes 12582916
  23.1 5.3 %copy-start.2 = (bf16[1,256,4096]{2,1,0:T(8,128)(2,1)S(1)}, bf16[1,256,4096]{2,1,0:T(8,128)(2,1)}, u32[]{:S(2)}) copy-start(bf16[1,256,4096]{2,1,0:T(8,128)(2,1)} %param.6) | copy-start | bytes 6291460
  31.1 7.9 %copy-start.4 = (s32[3]{0:T(128)S(1)}, s32[3]{0:T(128)}, u32[]{:S(2)}) copy-start(s32[3]{0:T(128)} %constant.69) | copy-start | bytes 40
  31.1 8.0 %copy-start.5 = (s32[3]{0:T(128)S(1)}, s32[3]{0:T(128)}, u32[]{:S(2)}) copy-start(s32[3]{0:T(128)} %constant.66) | copy-start | bytes 40
  109.1 279.5 %all-gather.2.cloned.1.call-start = ((), (), s32[]{:S(2)}) async-start(), calls=%async_computation.1 | async-start | bytes 6291456 | tf_op jit(solution)/shard_map/all_gather | solution.py:74
  311.9 8.1 %copy-start.3 = (bf16[256,4096]{1,0:T(8,128)(2,1)S(1)}, bf16[256,4096]{1,0:T(8,128)(2,1)}, u32[]{:S(2)}) copy-start(bf16[256,4096]{1,0:T(8,128)(2,1)} %param.4) | copy-start | bytes 6291460
  371.0 6.3 %copy-start = (bf16[4,64,64,64]{3,1,2,0:T(8,128)(2,1)S(1)}, bf16[4,64,64,64]{3,1,2,0:T(8,128)(2,1)}, u32[]{:S(2)}) copy-start(bf16[4,64,64,64]{3,1,2,0:T(8,128)(2,1)} %get-tuple-element.4) | copy-start | bytes 6291460
Sparse Core Ops, SparseCore 0:
  109.2 170.6 all-reduce.1
  324.2 55.9 all-gather.1
where the time goes:
time: 408 us; the launch traced here: 401 us
  waiting for transfers between devices  171 us (42%)
  local copies, waits for them, and re-layouts  76.6 us (19%)
  matrix products  71.4 us (18%)
  other arithmetic  67.1 us (16%)
  between operations  14.6 us (4%)
    psum x1, waiting for transfers between devices, per_device(): summed = lax.psum(fill_grid(picked, own_pos), 'replica')  171 us
    unnamed x4, other arithmetic  45.6 us
    dot_general x2, matrix products, decode(): jnp.einsum('ai,xyab,bj->xiyj', basis_table, square, basis_table, precisio...  23.9 us
    dot_general x1, matrix products, expand(): jnp.einsum('xyki,xyk,xykj->xiyj', left_rows, values, right_rows, precisio...  18.5 us
    dot_general x1, matrix products, extract(): jnp.einsum('xyki,xiyj->xykj', left_rows, block_view, precision=lax.Precis...  17.1 us
    mul x2, local copies, waits for them, and re-layouts, per_device(): step_rate * smooth  16.1 us
    dot_general x2, matrix products, basis_rows(): jnp.einsum('xyka,ai->xyki', one_hot, basis_table, precision=lax.Precision...  11.8 us
    convert_element_type x2, local copies, waits for them, and re-layouts, per_device(): direction = smooth.astype(jnp.bfloat16)  11.3 us
  transfers between devices with their start and end apart: 2, of which 1 were waited for; matrix products, arithmetic and copies ran while one was open for 16% of the time, Pallas kernels for 0%

commit v1 on v0

v1 whole, which is shorter than its diff:
```python
import functools
import math

import jax
import jax.numpy as jnp
import numpy as np
from jax import lax
from jax.experimental import pallas as pl
from jax.experimental.pallas import tpu as pltpu
from jax.sharding import PartitionSpec as P

GROUP = 64
LANES = 128
WIDE = 256

beta_decay = 0.9
step_rate = 0.02

f32, bf16 = jnp.float32, jnp.bfloat16
MESH = pl.DeviceIdType.MESH


def basis_parts(blocks, transposed):
    k = np.arange(GROUP, dtype=np.float64)[:, None]
    i = np.arange(GROUP, dtype=np.float64)[None, :]
    scale = np.where(k == 0, math.sqrt(1.0 / GROUP), math.sqrt(2.0 / GROUP))
    c = scale * np.cos(math.pi * (2.0 * i + 1.0) * k / (2.0 * GROUP))
    if transposed:
        c = c.T
    full = np.kron(np.eye(blocks), c).astype(np.float32)
    high = full.astype(bf16)
    low = (full - high.astype(np.float32)).astype(bf16)
    return np.stack([high, low])


def split(x):
    high = x.astype(bf16)
    return high, (x - high.astype(f32)).astype(bf16)


def dot(a, b):
    return jnp.dot(a, b, preferred_element_type=f32)


def dot_t(a, b):
    return lax.dot_general(a, b, (((1,), (1,)), ((), ())), preferred_element_type=f32)


def left(m, x):
    high, low = split(x)
    return dot(m[0], high) + (dot(m[0], low) + dot(m[1], high))


def right(x, m):
    high, low = split(x)
    return dot(high, m[0]) + (dot(low, m[0]) + dot(high, m[1]))


def down(rows):
    return lax.broadcasted_iota(jnp.int32, (rows, LANES), 0).astype(f32)


def lane_offset(topk):
    lane = lax.broadcasted_iota(jnp.int32, (1, LANES), 1)
    return (lane // topk * GROUP).astype(f32)


def place(pos, topk):
    a = jnp.floor(pos * (1.0 / GROUP))
    return a, pos - a * GROUP + lane_offset(topk)


def own_kernel(nx, topk, mom, grad, pos, lf, rt, li, ri, kept, sent):
    moved = beta_decay * mom[0] + grad[0].astype(f32)
    coeff = right(left(lf, moved), rt)
    spots = pos[0]
    a, b = place(spots, topk)
    rows, cols = down(GROUP), down(WIDE)
    picked, own = [], []
    for x in range(nx):
        part = coeff[x * GROUP : (x + 1) * GROUP]
        at_row = rows == a[x : x + 1]
        hot_a = jnp.where(at_row, 1.0, 0.0).astype(bf16)
        hot_b = jnp.where(cols == b[x : x + 1], 1.0, 0.0).astype(bf16)
        own.append(part * dot_t(hot_a, hot_b))
        high, low = split(part)
        found = dot(jnp.concatenate([high, low], axis=0), hot_b)
        found = found[:GROUP] + found[GROUP:]
        picked.append(jnp.sum(jnp.where(at_row, found, 0.0), axis=0, keepdims=True))
    kept[0] = moved - right(left(li, jnp.concatenate(own, axis=0)), ri)
    sent[0] = jnp.concatenate(picked + [spots], axis=0)


def own_part(mom, grad, pos, topk, interpret=False):
    _, rows, width = mom.shape
    nx = rows // GROUP
    steps = width // WIDE
    blocks = WIDE // GROUP
    whole = lambda n: pl.BlockSpec((2, n, n), lambda g: (0, 0, 0))
    return pl.pallas_call(
        functools.partial(own_kernel, nx, topk),
        grid=(steps,),
        in_specs=[
            pl.BlockSpec((1, rows, WIDE), lambda g: (0, 0, g)),
            pl.BlockSpec((1, rows, WIDE), lambda g: (0, 0, g)),
            pl.BlockSpec((1, nx, LANES), lambda g: (g, 0, 0)),
            whole(rows), whole(WIDE), whole(rows), whole(WIDE),
        ],
        out_specs=[
            pl.BlockSpec((1, rows, WIDE), lambda g: (0, 0, g)),
            pl.BlockSpec((1, 2 * nx, LANES), lambda g: (g, 0, 0)),
        ],
        out_shape=[
            jax.ShapeDtypeStruct((1, rows, width), f32),
            jax.ShapeDtypeStruct((steps, 2 * nx, LANES), f32),
        ],
        interpret=interpret,
        name="own_part",
    )(
        mom, grad, pos,
        basis_parts(nx, False), basis_parts(blocks, True),
        basis_parts(nx, True), basis_parts(blocks, False),
    )


def swap_kernel(reps, shards, mine, got, send_sem, recv_sem, own_sem):
    r, s = lax.axis_index("replica"), lax.axis_index("shard")
    me = r * shards + s
    total = reps * shards
    keep = pltpu.make_async_copy(mine.at[lax.rem(r, 2)], got.at[s, r], own_sem)
    keep.start()

    def push(step):
        to = lax.rem(me + step, total)
        to_r, to_s = to // shards, lax.rem(to, shards)
        return pltpu.make_async_remote_copy(
            src_ref=mine.at[lax.rem(to_r, 2)],
            dst_ref=got.at[s, r],
            send_sem=send_sem.at[step],
            recv_sem=recv_sem.at[step],
            device_id=(to_r, to_s),
            device_id_type=MESH,
        )

    def come(step):
        of = lax.rem(me - step + total, total)
        of_r, of_s = of // shards, lax.rem(of, shards)
        return pltpu.make_async_remote_copy(
            src_ref=mine.at[0],
            dst_ref=got.at[of_s, of_r],
            send_sem=send_sem.at[step],
            recv_sem=recv_sem.at[step],
            device_id=(of_r, of_s),
            device_id_type=MESH,
        )

    @pl.loop(1, total)
    def _(step):
        push(step).start()

    @pl.loop(1, total)
    def _(step):
        push(step).wait_send()
        come(step).wait_recv()

    keep.wait()


def swap(mine, reps, shards):
    return pl.pallas_call(
        functools.partial(swap_kernel, reps, shards),
        in_specs=[pl.BlockSpec(memory_space=pltpu.VMEM)],
        out_specs=pl.BlockSpec(memory_space=pltpu.VMEM),
        out_shape=jax.ShapeDtypeStruct((shards, reps) + mine.shape[1:], f32),
        scratch_shapes=[
            pltpu.SemaphoreType.DMA((reps * shards,)),
            pltpu.SemaphoreType.DMA((reps * shards,)),
            pltpu.SemaphoreType.DMA,
        ],
        compiler_params=pltpu.CompilerParams(has_side_effects=True),
        name="swap",
    )(mine)


def sum_kernel(nx, topk, reps, _, data, weight, li, ri, smooth_out, weight_out):
    rows, cols = down(GROUP), down(WIDE)
    tiles = []
    for x in range(nx):
        lefts, rights = [], []
        for r in range(reps):
            tile = data[0, r, 0]
            a, b = place(tile[nx + x : nx + x + 1], topk)
            high, low = split(tile[x : x + 1])
            at_row = rows == a
            lefts.append(jnp.concatenate([
                jnp.where(at_row, high.astype(f32), 0.0).astype(bf16),
                jnp.where(at_row, low.astype(f32), 0.0).astype(bf16),
            ], axis=0))
            rights.append(jnp.where(cols == b, 1.0, 0.0).astype(bf16))
        both = dot_t(jnp.concatenate(lefts, axis=1), jnp.concatenate(rights, axis=1))
        tiles.append(both[:GROUP] + both[GROUP:])
    smooth = jnp.tanh(right(left(li, jnp.concatenate(tiles, axis=0)), ri))
    smooth_out[...] = smooth.astype(bf16)
    weight_out[...] = (weight[...].astype(f32) - step_rate * smooth).astype(bf16)


def sum_part(shard, data, weight, topk, interpret=False):
    rows, width = weight.shape
    nx = rows // GROUP
    reps = data.shape[1]
    blocks = WIDE // GROUP
    column = pl.BlockSpec((rows, WIDE), lambda g, s: (0, g))
    whole = lambda n: pl.BlockSpec((2, n, n), lambda g, s: (0, 0, 0))
    return pl.pallas_call(
        functools.partial(sum_kernel, nx, topk, reps),
        grid_spec=pltpu.PrefetchScalarGridSpec(
            num_scalar_prefetch=1,
            grid=(width // WIDE,),
            in_specs=[
                pl.BlockSpec((1, reps, 1, 2 * nx, LANES), lambda g, s: (s[0], 0, g, 0, 0)),
                column, whole(rows), whole(WIDE),
            ],
            out_specs=[column, column],
        ),
        out_shape=[jax.ShapeDtypeStruct((rows, width), bf16)] * 2,
        interpret=interpret,
        name="sum_part",
    )(shard, data, weight, basis_parts(nx, True), basis_parts(blocks, False))


def per_device(reps, shards, weight, momentum, grad, positions):
    rows, width = weight.shape
    _, nx, ny, topk = positions.shape
    half = width // 2
    steps = width // WIDE
    r, s = lax.axis_index("replica"), lax.axis_index("shard")
    core = lax.rem(r, 2)

    mine_w = lax.dynamic_slice(weight, (0, core * half), (rows, half))
    weights = [mine_w] + [
        lax.ppermute(mine_w, "shard", [(i, (i + d) % shards) for i in range(shards)])
        for d in range(1, shards)
    ]

    pos = positions[0].astype(f32).reshape(nx, steps, LANES).transpose(1, 0, 2)
    kept, sent = own_part(momentum, grad, pos, topk)
    got = swap(sent.reshape(2, steps // 2, 2 * nx, LANES), reps, shards)

    pairs = [(i, i ^ 1) for i in range(reps)]
    flip = lambda x: lax.ppermute(x, "replica", pairs)
    order = lambda a, b: [jnp.where(core == 0, a, b), jnp.where(core == 0, b, a)]
    pieces, direction = [], None
    for d in range(shards):
        of = lax.rem(s - d + shards, shards)
        smooth, updated = sum_part(of.reshape(1).astype(jnp.int32), got, weights[d], topk)
        if d == 0:
            direction = jnp.concatenate(order(smooth, flip(smooth)), axis=1)
        pieces.append((updated, flip(updated)))

    columns = []
    for t in range(shards):
        d = lax.rem(s - t + shards, shards)
        a, b = pieces[0]
        for e in range(1, shards):
            a = jnp.where(d == e, pieces[e][0], a)
            b = jnp.where(d == e, pieces[e][1], b)
        columns += order(a, b)
    return (kept, direction, jnp.concatenate(columns, axis=1))


def solution(mesh):
    reps, shards = mesh.shape["replica"], mesh.shape["shard"]
    in_specs = (
        P(None, "shard"),
        P("replica", None, "shard"),
        P("replica", None, "shard"),
        P("replica", None, "shard", None),
    )
    out_specs = (P("replica", None, "shard"), P(None, "shard"), P())
    return jax.shard_map(
        functools.partial(per_device, reps, shards),
        mesh=mesh, in_specs=in_specs, out_specs=out_specs, check_vma=False,
    )
```

time: 408 us -> 107 us (0.26); the launches traced: 401 us -> 107 us
  waiting for transfers between devices: 171 us -> 0.01 us
  Pallas kernels: 0 us -> 94.5 us
  local copies, waits for them, and re-layouts: 76.6 us -> 2.47 us
  matrix products: 71.4 us -> 0 us
  other arithmetic: 67.1 us -> 8.03 us
  between operations: 14.6 us -> 0.72 us
    psum x1 -> x0, waiting for transfers between devices: 171 us -> none  [per_device(): summed = lax.psum(fill_grid(picked, own_pos), 'replica')]
    pallas_call x0 -> x4, Pallas kernels: none -> 94.5 us  [the longest x2 38.3 us: sum_part(): pl.pallas_call(functools.partial(sum_kernel, nx, topk, reps), grid_spec=p...]
    dot_general x6 -> x0, matrix products: 71.4 us -> none  [the longest x2 23.9 us: decode(): jnp.einsum('ai,xyab,bj->xiyj', basis_table, square, basis_table, precisio...]
    unnamed x4 -> x0, other arithmetic: 45.6 us -> none
    mul x2 -> x0, local copies, waits for them, and re-layouts: 16.1 us -> none  [per_device(): step_rate * smooth]
    reshape x2 -> x0, local copies, waits for them, and re-layouts: 14.8 us -> none  [the longest x1 7.88 us: expand(): return dense.reshape(row_blocks * GROUP, col_blocks * GROUP)]
    dot_general x2 -> x0, local copies, waits for them, and re-layouts: 12.7 us -> none  [the longest x1 6.46 us: expand(): jnp.einsum('xyki,xyk,xykj->xiyj', left_rows, values, right_rows, precisio...]
    convert_element_type x2 -> x3, local copies, waits for them, and re-layouts: 11.3 us -> 0.81 us  [per_device(): pos = positions[0].astype(f32).reshape(nx, steps, LANES).transpose(1, 0, 2)]
  transfers between devices with their start and end apart: 2 -> 4, of which waited for: 1 -> 0; matrix products, arithmetic and copies ran while one was open for 16% -> 5% of each run, Pallas kernels for 0% -> 89%
where the time goes in v1:
time: 107 us
  Pallas kernels  94.5 us (88%)
  other arithmetic  8.03 us (8%)
  local copies, waits for them, and re-layouts  2.47 us (2%)
    pallas_call x2, Pallas kernels, sum_part(): pl.pallas_call(functools.partial(sum_kernel, nx, topk, reps), grid_spec=p...  38.3 us
    pallas_call x1, Pallas kernels, swap(): pl.pallas_call(functools.partial(swap_kernel, reps, shards), in_specs=[pl...  34.3 us
    pallas_call x1, Pallas kernels, own_part(): pl.pallas_call(functools.partial(own_kernel, nx, topk), grid=(steps,), in...  21.9 us
    select_n x2, other arithmetic, per_device(): jnp.where(core == 0, a, b)  3.38 us
    concatenate x1, other arithmetic, per_device(): return (kept, direction, jnp.concatenate(columns, axis=1))  2.23 us
  transfers between devices with their start and end apart: 4, of which 0 were waited for; matrix products, arithmetic and copies ran while one was open for 5% of the time, Pallas kernels for 89%

profile of v1, /device:TPU:15, one launch (start us, length us, event | category | flops | bytes accessed | tf_op | source)
XLA Modules:
  0.0 106.7 jit_solution(17722004219141447098)
XLA Ops:
  0.6 0.0 copy-start
  0.7 1.6 %copy-done = bf16[256,4096]{1,0:T(8,128)(2,1)S(1)} copy-done((bf16[256,4096]{1,0:T(8,128)(2,1)S(1)}, bf16[256,4096]{1,0:T(8,128)(2,1)}, u32[]{:S(2)}) %copy-start) | copy-done | bytes 2097176
  2.2 0.1 constant_dynamic-slice_fusion.weight
  2.3 0.0 copy-start.1
  2.3 0.3 collective-permute-start.1
  2.6 0.9 convert_element_type.7
  3.5 0.1 copy.15
  3.6 0.1 convert_element_type.8
  3.7 0.6 copy.18
  4.3 21.9 %own_part.1 = (f32[1,256,4096]{2,1,0:T(8,128)}, f32[16,8,128]{2,1,0:T(8,128)}) custom-call(f32[1,256,4096]{2,1,0:T(8,128)} %mom.1, bf16[1,256,4096]{2,1,0:T(8,128)(2,1)} %grad.1, f32[16,4,128]{2,1,0:T(4,128)} %bitcast.8, bf16[2,256,256]{2,1,0:T(8,128)(2,1)} %constant.30.clone.lf.ri, bf16[2,256,256]{2,1,0:T(8,128)(2,1)} %constant.31.clone.rt.li, ...), custom_call_target="tpu_custom_call" | custom-call | tf_op jit(solution)/shard_map/own_part/pallas_call | solution.py:100
  26.3 34.3 %swap.1.data = f32[2,16,8,8,128]{4,3,2,1,0:T(8,128)} custom-call(f32[2,8,8,128]{3,2,1,0:T(8,128)} %bitcast.9), custom_call_target="tpu_custom_call" | custom-call | tf_op jit(solution)/shard_map/swap/pallas_call | solution.py:170
  60.6 0.0 copy-done.1
  60.6 19.1 %sum_part.2 = (bf16[256,2048]{1,0:T(8,128)(2,1)}, bf16[256,2048]{1,0:T(8,128)(2,1)}) custom-call(s32[1]{0:T(128)} %bitcast.1._, f32[2,16,8,8,128]{4,3,2,1,0:T(8,128)} %swap.1.data, bf16[256,2048]{1,0:T(8,128)(2,1)} %copy-done.1, bf16[2,256,256]{2,1,0:T(8,128)(2,1)} %constant.31.clone.rt.li, bf16[2,256,256]{2,1,0:T(8,128)(2,1)} %constant.30.clone.lf.ri), custom_call_target="tpu_custom_call" | custom-call | tf_op jit(solution)/shard_map/sum_part/pallas_call | solution.py:214
  79.8 0.0 collective-permute-start
  79.8 0.5 collective-permute-start.3
  80.3 0.0 collective-permute-done.1.weight
  80.3 19.1 %sum_part.3 = (bf16[256,2048]{1,0:T(8,128)(2,1)}, bf16[256,2048]{1,0:T(8,128)(2,1)}) custom-call(s32[1]{0:T(128)} %bitcast.3._, f32[2,16,8,8,128]{4,3,2,1,0:T(8,128)} %swap.1.data, bf16[256,2048]{1,0:T(8,128)(2,1)} %collective-permute-done.1.weight, bf16[2,256,256]{2,1,0:T(8,128)(2,1)} %constant.31.clone.rt.li, bf16[2,256,256]{2,1,0:T(8,128)(2,1)} %constant.30.clone.lf.ri), custom_call_target="tpu_custom_call" | custom-call | tf_op jit(solution)/shard_map/sum_part/pallas_call | solution.py:214
  99.4 0.0 copy-start.2
  99.4 0.0 copy-start.3
  99.4 0.1 collective-permute-start.2
  99.5 0.0 collective-permute-done
  99.6 1.8 %broadcast_select_fusion.9 = (bf16[256,2048]{1,0:T(8,128)(2,1)S(1)}, bf16[256,2048]{1,0:T(8,128)(2,1)S(1)}) fusion(bf16[256,2048]{1,0:T(8,128)(2,1)} %get-tuple-element.10, bf16[256,2048]{1,0:T(8,128)(2,1)} %collective-permute-done, pred[]{:T(512)S(6)} %eq.6), kind=kLoop, calls=%fused_computation.11 | loop fusion | flops 1048576 | bytes 4194305 | tf_op jit(solution)/shard_map/jit(_where)/select_n | solution.py:251
  101.4 1.5 %pad_maximum_fusion.1 = bf16[256,4096]{1,0:T(8,128)(2,1)} fusion(bf16[256,2048]{1,0:T(8,128)(2,1)S(1)} %get-tuple-element.18, bf16[256,2048]{1,0:T(8,128)(2,1)S(1)} %get-tuple-element.17), kind=kLoop, calls=%fused_computation.1 | loop fusion | flops 4194304 | bytes 4194304 | tf_op jit(solution)/shard_map/concatenate | solution.py:257
  102.9 0.0 collective-permute-done.3
  102.9 0.0 collective-permute-done.2
  102.9 0.0 copy-done.2
  102.9 0.0 copy-done.3
  102.9 1.6 %broadcast_select_fusion.7 = (bf16[256,2048]{1,0:T(8,128)(2,1)S(1)}, bf16[256,2048]{1,0:T(8,128)(2,1)S(1)}, bf16[256,2048]{1,0:T(8,128)(2,1)S(1)}, bf16[256,2048]{1,0:T(8,128)(2,1)S(1)}) fusion(pred[]{:T(512)S(6)} %eq.6, bf16[256,2048]{1,0:T(8,128)(2,1)S(1)} %copy-done.3, bf16[256,2048]{1,0:T(8,128)(2,1)S(1)} %copy-done.2, pred[]{:T(512)S(6)} %eq.7, ...), kind=kLoop, calls=%fused_computation.9 | loop fusion | flops 4194304 | bytes 8388611 | tf_op jit(solution)/shard_map/jit(_where)/select_n | solution.py:251
  104.5 2.2 %pad_maximum_fusion = bf16[256,8192]{1,0:T(8,128)(2,1)} fusion(bf16[256,2048]{1,0:T(8,128)(2,1)S(1)} %get-tuple-element.16, bf16[256,2048]{1,0:T(8,128)(2,1)S(1)} %get-tuple-element.15, bf16[256,2048]{1,0:T(8,128)(2,1)S(1)} %get-tuple-element.14, bf16[256,2048]{1,0:T(8,128)(2,1)S(1)} %get-tuple-element.13), kind=kLoop, calls=%fused_computation | loop fusion | flops 16777216 | bytes 8388608 | tf_op jit(solution)/shard_map/concatenate | solution.py:268
Async XLA Ops:
  0.6 1.6 %copy-start = (bf16[256,4096]{1,0:T(8,128)(2,1)S(1)}, bf16[256,4096]{1,0:T(8,128)(2,1)}, u32[]{:S(2)}) copy-start(bf16[256,4096]{1,0:T(8,128)(2,1)} %param.12) | copy-start | bytes 6291460
  2.3 58.3 %copy-start.1 = (bf16[256,2048]{1,0:T(8,128)(2,1)}, bf16[256,2048]{1,0:T(8,128)(2,1)S(1)}, u32[]{:S(2)}) copy-start(bf16[256,2048]{1,0:T(8,128)(2,1)S(1)} %constant_dynamic-slice_fusion.weight) | copy-start | bytes 3145732
  2.3 78.0 %collective-permute-start.1 = (bf16[256,2048]{1,0:T(8,128)(2,1)S(1)}, bf16[256,2048]{1,0:T(8,128)(2,1)}, u32[]{:S(2)}, u32[]{:S(2)}) collective-permute-start(bf16[256,2048]{1,0:T(8,128)(2,1)S(1)} %constant_dynamic-slice_fusion.weight), channel_id=1, source_target_pairs={{0,1},{1,0},{2,3},{3,2},{4,5},{5,4},{6,7},{7,6},{8,9},{9,8},{10,11... | collective-permute-start | bytes 3145736 | tf_op jit(solution)/shard_map/ppermute | solution.py:241
  79.8 19.8 %collective-permute-start = (bf16[256,2048]{1,0:T(8,128)(2,1)}, bf16[256,2048]{1,0:T(8,128)(2,1)}, u32[]{:S(2)}, u32[]{:S(2)}) collective-permute-start(bf16[256,2048]{1,0:T(8,128)(2,1)} %get-tuple-element.10), channel_id=1, source_target_pairs={{0,2},{2,0},{4,6},{6,4},{8,10},{10,8},{12,14},{14,12},{16,18},{18,... | collective-permute-start | bytes 3145736 | tf_op jit(solution)/shard_map/ppermute | solution.py:250
  79.8 23.1 %collective-permute-start.3 = (bf16[256,2048]{1,0:T(8,128)(2,1)}, bf16[256,2048]{1,0:T(8,128)(2,1)}, u32[]{:S(2)}, u32[]{:S(2)}) collective-permute-start(bf16[256,2048]{1,0:T(8,128)(2,1)} %get-tuple-element.12), channel_id=1, source_target_pairs={{0,2},{2,0},{4,6},{6,4},{8,10},{10,8},{12,14},{14,12},{16,18},{18,... | collective-permute-start | bytes 3145736 | tf_op jit(solution)/shard_map/ppermute | solution.py:250
  99.4 3.5 %copy-start.2 = (bf16[256,2048]{1,0:T(8,128)(2,1)S(1)}, bf16[256,2048]{1,0:T(8,128)(2,1)}, u32[]{:S(2)}) copy-start(bf16[256,2048]{1,0:T(8,128)(2,1)} %get-tuple-element.12) | copy-start | bytes 3145732
  99.4 3.5 %copy-start.3 = (bf16[256,2048]{1,0:T(8,128)(2,1)S(1)}, bf16[256,2048]{1,0:T(8,128)(2,1)}, u32[]{:S(2)}) copy-start(bf16[256,2048]{1,0:T(8,128)(2,1)} %get-tuple-element.11) | copy-start | bytes 3145732
  99.4 3.5 %collective-permute-start.2 = (bf16[256,2048]{1,0:T(8,128)(2,1)}, bf16[256,2048]{1,0:T(8,128)(2,1)S(1)}, u32[]{:S(2)}, u32[]{:S(2)}) collective-permute-start(bf16[256,2048]{1,0:T(8,128)(2,1)} %get-tuple-element.11), channel_id=1, source_target_pairs={{0,2},{2,0},{4,6},{6,4},{8,10},{10,8},{12,14},{14,12},{16,18},{18,... | collective-permute-start | bytes 3145736 | tf_op jit(solution)/shard_map/ppermute | solution.py:250
